TPU v7x, 32 devices: a whole 2x2x4 slice. The times are simulated.
32 devices in a mesh: dom: 16 (over z, y, x), mem: 2 (over core).
Axes of the slice: x: 2, y: 2, z: 4, core: 2. Of those that a mesh axis runs over, the one named last changes fastest.
Arguments:
- node_latents: bfloat16 [4, 2048, 512], P('mem', 'dom'), may hold values from -6 to 6
- edge_latents: bfloat16 [4, 8192, 512], P('mem', 'dom'), may hold values from -6 to 6
- edge_senders: int32 [8192], P('dom'), may hold values from 0 to 191, as said below
- edge_receivers: int32 [8192], P('dom'), may hold values from 0 to 127
- edge_counts: int32 [16], P('dom'), may hold values from 64 to 512, as said below
- halo_send: int32 [512], P('dom'), may hold values from 0 to 127
- long_send: int32 [16, 16, 2], replicated, may hold values from 0 to 3
- edge_first: bfloat16 [2, 1536, 512], P(None, None, 'mem'), may hold values from -0.15625 to 0.15625
- edge_second: bfloat16 [2, 512, 512], P(None, None, 'mem'), may hold values from -0.25 to 0.25
- node_first: bfloat16 [2, 1024, 512], P(None, None, 'mem'), may hold values from -0.1875 to 0.1875
- node_second: bfloat16 [2, 512, 512], P(None, None, 'mem'), may hold values from -0.25 to 0.25
- edge_gain: float32 [2, 512], replicated, may hold values from 0.5 to 1.5
- edge_shift: float32 [2, 512], replicated, may hold values from -3 to 3
- node_gain: float32 [2, 512], replicated, may hold values from 0.5 to 1.5
- node_shift: float32 [2, 512], replicated, may hold values from -3 to 3
Outputs:
- node_out: bfloat16 [4, 2048, 512], P('mem', 'dom')
- edge_out: bfloat16 [4, 8192, 512], P('mem', 'dom')
Inputs may be any that keep to these rules, and one draw needn't show every extreme that they name: `edge_senders`: rows below 128 are the partition's own nodes, the next 32 its neighbours' sent nodes, the rest the coarse slots of all partitions. `edge_counts`: live slots come first in each partition; some partition has exactly 512 live slots.
All inputs are finite; a program needn't handle non-finite values.
Results may differ from a plain program's by a relative error of at most 0.0075.
Values may be sent and summed in bfloat16 or wider, within the bound.
A program may use at most 128 MiB of HBM per device.

v0:
```python
import jax
import jax.numpy as jnp
from jax import lax
from jax.sharding import PartitionSpec as P

HALO = 16
LAYERS = 2


def with_halo(block, sides, width):
    for axis, dim in sides:
        count = lax.axis_size(axis)
        forward = [(i, i + 1) for i in range(count - 1)]
        forward.append((count - 1, 0))
        backward = [(target, source) for source, target in forward]
        low = lax.ppermute(
            lax.slice_in_dim(block, block.shape[dim] - width, None, axis=dim), axis, forward
        )
        high = lax.ppermute(lax.slice_in_dim(block, 0, width, axis=dim), axis, backward)
        block = jnp.concatenate([low, block, high], axis=dim)
    return block


def project_norm(inputs, first_weight, second, scale_gain, offset):
    hidden = jax.nn.silu(jnp.dot(inputs, first_weight, preferred_element_type=jnp.float32)).astype(
        jnp.bfloat16
    )
    output = jnp.dot(hidden, second, preferred_element_type=jnp.float32)
    average = jnp.mean(output, -1, keepdims=True)
    centred = output - average
    variance = jnp.mean(centred * centred, -1, keepdims=True)
    return centred * lax.rsqrt(variance + 1e-05) * scale_gain + offset


def per_device(
    node_latents,
    edge_latents,
    edge_senders,
    edge_receivers,
    edge_counts,
    halo_send,
    long_send,
    edge_first,
    edge_second,
    node_first,
    node_second,
    edge_gain,
    edge_shift,
    node_gain,
    node_shift,
):
    members, node_rows, features = node_latents.shape
    edge_rows = edge_latents.shape[1]
    position = lax.axis_index("dom")
    live_count = edge_counts[0]
    live_mask = jnp.arange(edge_rows, dtype=jnp.int32) < live_count
    onehot = (
        (edge_receivers[None, :] == jnp.arange(node_rows, dtype=jnp.int32)[:, None])
        & live_mask[None, :]
    ).astype(jnp.bfloat16)
    node_state = node_latents
    edge_state = edge_latents
    for layer_index in range(LAYERS):
        edge_inner, edge_outer, node_inner, node_outer = (
            lax.all_gather(edge_first[layer_index], "mem", axis=1, tiled=True),
            lax.all_gather(edge_second[layer_index], "mem", axis=1, tiled=True),
            lax.all_gather(node_first[layer_index], "mem", axis=1, tiled=True),
            lax.all_gather(node_second[layer_index], "mem", axis=1, tiled=True),
        )
        outgoing = jnp.take(node_state, halo_send, axis=1)
        bordered = with_halo(outgoing, (("dom", 1),), HALO)
        from_left = bordered[:, :HALO]
        from_right = bordered[:, 3 * HALO :]
        send_rows = lax.dynamic_index_in_dim(long_send, position, 0, keepdims=False).reshape(-1)
        packed = jnp.take(node_state, send_rows, axis=1)
        far_rows = lax.all_to_all(packed, "dom", split_axis=1, concat_axis=1, tiled=True)
        sources = jnp.concatenate([node_state, from_left, from_right, far_rows], 1)
        sender_rows = jnp.take(sources, edge_senders, axis=1)
        receiver_rows = jnp.take(node_state, edge_receivers, axis=1)
        joined = jnp.concatenate([edge_state, sender_rows, receiver_rows], -1)
        update = project_norm(
            joined.reshape(members * edge_rows, 3 * features),
            edge_inner,
            edge_outer,
            edge_gain[layer_index],
            edge_shift[layer_index],
        ).reshape(members, edge_rows, features)
        new_edges = jnp.where(
            live_mask[None, :, None], edge_state.astype(jnp.float32) + update, 0.0
        ).astype(jnp.bfloat16)
        summed = jnp.einsum(
            "ne,med->mnd", onehot, new_edges, preferred_element_type=jnp.float32
        ).astype(jnp.bfloat16)
        node_in = jnp.concatenate([node_state, summed], -1).reshape(
            members * node_rows, 2 * features
        )
        node_update = project_norm(
            node_in, node_inner, node_outer, node_gain[layer_index], node_shift[layer_index]
        ).reshape(members, node_rows, features)
        node_state = (node_state.astype(jnp.float32) + node_update).astype(jnp.bfloat16)
        edge_state = new_edges
    return (node_state, edge_state)


def solution(mesh):
    placed = (
        P("mem", "dom", None),
        P("mem", "dom", None),
        P("dom"),
        P("dom"),
        P("dom"),
        P("dom"),
        P(),
        P(None, None, "mem"),
        P(None, None, "mem"),
        P(None, None, "mem"),
        P(None, None, "mem"),
        P(),
        P(),
        P(),
        P(),
    )
    return jax.shard_map(
        per_device,
        mesh=mesh,
        in_specs=placed,
        out_specs=(P("mem", "dom", None), P("mem", "dom", None)),
        check_vma=False,
    )
```

profile of v0, /device:TPU:0, one launch (start us, length us, event | category | flops | bytes accessed | tf_op | source)
XLA Modules:
  0.0 136.8 jit_solution(4153508605069682487)
XLA Ops:
  7.2 2.7 %fusion.60 = (bf16[1,1536,256]{2,1,0:T(8,128)(2,1)}, bf16[1,1536,256]{2,1,0:T(8,128)(2,1)}) fusion(bf16[2,1536,256]{2,1,0:T(8,128)(2,1)} %param.28), kind=kLoop, calls=%fused_computation.105 | loop fusion | bytes 3145728 | tf_op jit(solution)/shard_map/slice | solution.py:65
  10.1 1.1 fusion.61
  11.2 0.7 all-gather.17.cloned.1.call-update
  12.2 0.8 gather_fusion.1
  13.0 0.7 copy.84
  13.7 8.3 %all-to-all-start = ((bf16[2,32,512]{2,0,1:T(2,128)(2,1)}), bf16[2,32,512]{2,0,1:T(2,128)(2,1)S(1)}, u32[]{:S(2)}, u32[]{:S(2)}) async-start(bf16[2,32,512]{2,0,1:T(2,128)(2,1)} %copy.84), calls=%async_computation | async-start | bytes 131072 | tf_op jit(solution)/shard_map/all_to_all | solution.py:76
  22.2 0.8 gather_fusion
  23.0 2.0 %collective-permute-start = (bf16[2,16,512]{2,1,0:T(8,128)(2,1)S(1)}, bf16[2,16,512]{2,1,0:T(8,128)(2,1)S(1)}, u32[]{:S(2)}, u32[]{:S(2)}) collective-permute-start(bf16[2,16,512]{2,1,0:T(8,128)(2,1)S(1)} %get-tuple-element.23), channel_id=1, source_target_pairs={{0,2},{2,4},{4,6},{6,8},{8,10},{10,12},{12,14},{14,16},{16,18},{18... | collective-permute-start | bytes 98312 | tf_op jit(solution)/shard_map/ppermute | solution.py:16
  25.0 3.7 %collective-permute-start.1 = (bf16[2,16,512]{2,1,0:T(8,128)(2,1)S(1)}, bf16[2,16,512]{2,1,0:T(8,128)(2,1)S(1)}, u32[]{:S(2)}, u32[]{:S(2)}) collective-permute-start(bf16[2,16,512]{2,1,0:T(8,128)(2,1)S(1)} %get-tuple-element.24), channel_id=1, source_target_pairs={{2,0},{4,2},{6,4},{8,6},{10,8},{12,10},{14,12},{16,14},{18,16},{20... | collective-permute-start | bytes 98312 | tf_op jit(solution)/shard_map/ppermute | solution.py:19
  28.9 4.4 %gather_fusion.3 = bf16[512,2,512]{2,0,1:T(8,128)(2,1)S(1)} fusion(bf16[2,128,512]{2,1,0:T(8,128)(2,1)S(1)} %copy-done.1, s32[1024]{0:T(1024)S(1)} %pad_clamp_fusion), kind=kCustom, calls=%fused_computation.2.clone | custom fusion | bytes 2099200 | tf_op jit(solution)/shard_map/jit(_take)/gather | solution.py:79
  33.4 2.4 %all-gather.1 = bf16[1,512,512]{2,1,0:T(8,128)(2,1)} all-gather(bf16[1,512,256]{2,1,0:T(8,128)(2,1)S(1)} %get-tuple-element.18), channel_id=3, replica_groups=mesh['dom'=16,'mem'=2] {'mem'}, dimensions={2}, use_global_device_ids=true | all-gather | bytes 786432 | tf_op jit(solution)/shard_map/all_gather | solution.py:66
  35.9 2.3 %all-gather.3 = bf16[1,512,512]{2,1,0:T(8,128)(2,1)} all-gather(bf16[1,512,256]{2,1,0:T(8,128)(2,1)S(1)} %get-tuple-element.19), channel_id=5, replica_groups=mesh['dom'=16,'mem'=2] {'mem'}, dimensions={2}, use_global_device_ids=true | all-gather | bytes 786432 | tf_op jit(solution)/shard_map/all_gather | solution.py:68
  38.3 2.3 %all-gather.5 = bf16[1,512,512]{2,1,0:T(8,128)(2,1)} all-gather(bf16[1,512,256]{2,1,0:T(8,128)(2,1)S(1)} %get-tuple-element.17), channel_id=7, replica_groups=mesh['dom'=16,'mem'=2] {'mem'}, dimensions={2}, use_global_device_ids=true | all-gather | bytes 786432 | tf_op jit(solution)/shard_map/all_gather | solution.py:66
  40.6 2.6 %all-gather.7 = bf16[1,512,512]{2,1,0:T(8,128)(2,1)} all-gather(bf16[1,512,256]{2,1,0:T(8,128)(2,1)S(1)} %get-tuple-element.20), channel_id=9, replica_groups=mesh['dom'=16,'mem'=2] {'mem'}, dimensions={2}, use_global_device_ids=true | all-gather | bytes 786432 | tf_op jit(solution)/shard_map/all_gather | solution.py:68
  43.2 5.0 %fusion.29 = bf16[2,512,512]{2,0,1:T(2,128)(2,1)} fusion(bf16[512,2,512]{2,0,1:T(8,128)(2,1)S(1)} %gather_fusion.3, pred[512]{0:T(512)(128)(4,1)S(1)} %compare_and_fusion), kind=kLoop, calls=%fused_computation.45 | loop fusion | flops 524288 | bytes 2097664 | tf_op jit(solution)/shard_map/jit(_take)/select_n | solution.py:79
  49.3 2.1 %copy.82 = bf16[2,512,512]{2,0,1:T(2,128)(2,1)} copy(bf16[2,512,512]{2,1,0:T(8,128)(2,1)S(1)} %copy-done.2) | data formatting | bytes 2097152 | tf_op args[1]
  51.5 0.6 pad_maximum_fusion.5
  52.1 3.6 %gather_fusion.2 = bf16[512,2,512]{2,1,0:T(2,128)(2,1)S(1)} fusion(bf16[2,192,512]{2,0,1:T(2,128)(2,1)S(1)} %pad_maximum_fusion.5, s32[1024]{0:T(1024)S(1)} %pad_clamp_fusion.1), kind=kCustom, calls=%fused_computation.1.clone | custom fusion | bytes 2099200 | tf_op jit(solution)/shard_map/jit(_take)/gather | solution.py:78
  55.7 2.0 %fusion.27 = bf16[2,512,512]{2,0,1:T(2,128)(2,1)S(1)} fusion(bf16[512,2,512]{2,1,0:T(2,128)(2,1)S(1)} %gather_fusion.2, pred[512]{0:T(512)(128)(4,1)S(1)} %compare_and_fusion.1), kind=kLoop, calls=%fused_computation.43 | loop fusion | flops 524288 | bytes 2097664 | tf_op jit(solution)/shard_map/jit(_take)/select_n | solution.py:78
  57.7 3.3 %pad_maximum_fusion = bf16[2,512,1536]{2,0,1:T(2,128)(2,1)S(1)} fusion(bf16[2,512,512]{2,0,1:T(2,128)(2,1)S(1)} %copy-done.4, bf16[2,512,512]{2,0,1:T(2,128)(2,1)S(1)} %fusion.27, bf16[2,512,512]{2,0,1:T(2,128)(2,1)S(1)} %copy-done.6), kind=kLoop, calls=%fused_computation.8 | loop fusion | flops 9437184 | bytes 6291456 | tf_op jit(solution)/shard_map/concatenate | solution.py:80
  61.0 2.1 %copy.90 = bf16[2,512,1536]{2,1,0:T(8,128)(2,1)} copy(bf16[2,512,1536]{2,0,1:T(2,128)(2,1)S(1)} %pad_maximum_fusion) | data formatting | bytes 6291456 | tf_op jit(solution)/shard_map/concatenate | solution.py:80
  63.1 5.0 %fusion.70 = (f32[1024]{0:T(1024)S(1)}, f32[1024,512]{1,0:T(8,128)S(1)}) fusion(bf16[1,512,512]{2,1,0:T(8,128)(2,1)} %all-gather.1, bf16[1024,1536]{1,0:T(8,128)(2,1)} %bitcast.105, bf16[1,1536,512]{2,1,0:T(8,128)(2,1)} %all-gather.13.cloned.1.call-done), kind=kOutput, calls=%fused_computation.115 | convolution fusion | flops 2150628352 | bytes 7344128 | tf_op jit(solution)/shard_map/dot_general | solution.py:28
  68.1 0.4 multiply_reduce_fusion.1
  68.9 5.5 %fusion.3 = bf16[2,512,512]{2,0,1:T(2,128)(2,1)S(1)} fusion(f32[2,512,512]{2,1,0:T(8,128)S(1)} %bitcast.104, pred[512]{0:T(512)(128)(4,1)S(1)} %iota_compare_fusion.1, bf16[2,512,512]{2,1,0:T(8,128)(2,1)S(1)} %copy-done.2), kind=kLoop, calls=%fused_computation.15 | loop fusion | flops 2097152 | bytes 4194816 | tf_op jit(solution)/shard_map/convert_element_type | solution.py:90
  74.4 0.5 fusion.18
  75.5 2.0 %fusion.73 = (f32[256]{0:T(256)S(1)}, f32[256,512]{1,0:T(8,128)S(1)}) fusion(bf16[1,512,512]{2,1,0:T(8,128)(2,1)S(1)} %copy-done.11, bf16[256,1024]{1,0:T(8,128)(2,1)S(1)} %bitcast.109, bf16[1,1024,512]{2,1,0:T(8,128)(2,1)} %all-gather.15.cloned.1.call-done), kind=kOutput, calls=%fused_computation.116 | convolution fusion | flops 403439360 | bytes 2622464 | tf_op jit(solution)/shard_map/dot_general | solution.py:28
  78.7 0.7 gather_fusion.4
  79.4 0.7 gather_fusion.5
  80.1 3.6 %gather_fusion.7 = bf16[512,2,512]{2,1,0:T(2,128)(2,1)S(1)} fusion(bf16[2,128,512]{2,0,1:T(2,128)(2,1)S(1)} %copy.96, s32[1024]{0:T(1024)S(1)} %pad_clamp_fusion), kind=kCustom, calls=%fused_computation.7.clone | custom fusion | bytes 2099200 | tf_op jit(solution)/shard_map/jit(_take)/gather | solution.py:79
  83.9 0.8 fusion.64
  84.7 5.6 %collective-permute-start.3 = (bf16[2,16,512]{1,2,0:T(8,128)(2,1)S(1)}, bf16[2,16,512]{1,2,0:T(8,128)(2,1)}, u32[]{:S(2)}, u32[]{:S(2)}) collective-permute-start(bf16[2,16,512]{1,2,0:T(8,128)(2,1)S(1)} %get-tuple-element.22), channel_id=1, source_target_pairs={{2,0},{4,2},{6,4},{8,6},{10,8},{12,10},{14,12},{16,14},{18,16},{20... | collective-permute-start | bytes 98312 | tf_op jit(solution)/shard_map/ppermute | solution.py:19
  90.3 0.7 fusion.55
  91.1 3.5 %all-to-all-start.1 = ((bf16[2,32,512]{2,0,1:T(2,128)(2,1)}), bf16[2,32,512]{2,0,1:T(2,128)(2,1)S(1)}, u32[]{:S(2)}, u32[]{:S(2)}) async-start(bf16[2,32,512]{2,0,1:T(2,128)(2,1)} %fusion.55), calls=%async_computation.1 | async-start | bytes 131072 | tf_op jit(solution)/shard_map/all_to_all | solution.py:76
  94.6 2.6 %fusion.30 = bf16[2,512,512]{2,0,1:T(2,128)(2,1)} fusion(bf16[512,2,512]{2,1,0:T(2,128)(2,1)S(1)} %gather_fusion.7, pred[512]{0:T(512)(128)(4,1)S(1)} %compare_and_fusion), kind=kLoop, calls=%fused_computation.46 | loop fusion | flops 524288 | bytes 2097664 | tf_op jit(solution)/shard_map/jit(_take)/select_n | solution.py:79
  97.2 4.9 %all-to-all-done.1 = bf16[2,32,512]{2,0,1:T(2,128)(2,1)S(1)} async-done(((bf16[2,32,512]{2,0,1:T(2,128)(2,1)}), bf16[2,32,512]{2,0,1:T(2,128)(2,1)S(1)}, u32[]{:S(2)}, u32[]{:S(2)}) %all-to-all-start.1) | async-done | bytes 65568 | tf_op jit(solution)/shard_map/all_to_all | solution.py:76
  102.3 1.2 pad_maximum_fusion.3
  103.5 0.5 copy.100
  104.0 3.6 %gather_fusion.6 = bf16[512,2,512]{2,1,0:T(2,128)(2,1)S(1)} fusion(bf16[2,192,512]{2,0,1:T(2,128)(2,1)S(1)} %copy.100, s32[1024]{0:T(1024)S(1)} %pad_clamp_fusion.1), kind=kCustom, calls=%fused_computation.6.clone | custom fusion | bytes 2099200 | tf_op jit(solution)/shard_map/jit(_take)/gather | solution.py:78
  107.6 2.0 %fusion.28 = bf16[2,512,512]{2,0,1:T(2,128)(2,1)S(1)} fusion(bf16[512,2,512]{2,1,0:T(2,128)(2,1)S(1)} %gather_fusion.6, pred[512]{0:T(512)(128)(4,1)S(1)} %compare_and_fusion.1), kind=kLoop, calls=%fused_computation.44 | loop fusion | flops 524288 | bytes 2097664 | tf_op jit(solution)/shard_map/jit(_take)/select_n | solution.py:78
  109.6 3.3 %pad_maximum_fusion.1 = bf16[2,512,1536]{2,0,1:T(2,128)(2,1)S(1)} fusion(bf16[2,512,512]{2,0,1:T(2,128)(2,1)S(1)} %copy-done.5, bf16[2,512,512]{2,0,1:T(2,128)(2,1)S(1)} %fusion.28, bf16[2,512,512]{2,0,1:T(2,128)(2,1)S(1)} %fusion.3), kind=kLoop, calls=%fused_computation.9 | loop fusion | flops 9437184 | bytes 6291456 | tf_op jit(solution)/shard_map/concatenate | solution.py:80
  112.9 2.1 %copy.102 = bf16[2,512,1536]{2,1,0:T(8,128)(2,1)} copy(bf16[2,512,1536]{2,0,1:T(2,128)(2,1)S(1)} %pad_maximum_fusion.1) | data formatting | bytes 6291456 | tf_op jit(solution)/shard_map/concatenate | solution.py:80
  115.0 5.0 %fusion.76 = (f32[1024]{0:T(1024)S(1)}, f32[1024,512]{1,0:T(8,128)S(1)}) fusion(bf16[1,512,512]{2,1,0:T(8,128)(2,1)} %all-gather.5, bf16[1024,1536]{1,0:T(8,128)(2,1)} %bitcast.106, bf16[1,1536,512]{2,1,0:T(8,128)(2,1)} %all-gather.17.cloned.1.call-done), kind=kOutput, calls=%fused_computation.117 | convolution fusion | flops 2150628352 | bytes 7344128 | tf_op jit(solution)/shard_map/dot_general | solution.py:28
  120.0 0.4 multiply_reduce_fusion
  120.8 4.3 %fusion.1 = bf16[2,512,512]{2,0,1:T(2,128)(2,1)S(1)} fusion(f32[2,512,512]{2,1,0:T(8,128)S(1)} %bitcast.103, bf16[2,512,512]{2,0,1:T(2,128)(2,1)S(1)} %fusion.3, pred[512]{0:T(512)(128)(4,1)S(1)} %iota_compare_fusion.1), kind=kLoop, calls=%fused_computation.12 | loop fusion | flops 2097152 | bytes 4194816 | tf_op jit(solution)/shard_map/convert_element_type | solution.py:90
  125.3 0.5 fusion.19
  126.1 0.6 copy-done.10
  126.7 2.0 %fusion.79 = (f32[256]{0:T(256)S(1)}, f32[256,512]{1,0:T(8,128)S(1)}) fusion(bf16[1,512,512]{2,1,0:T(8,128)(2,1)S(1)} %copy-done.10, bf16[256,1024]{1,0:T(8,128)(2,1)S(1)} %bitcast.110, bf16[1,1024,512]{2,1,0:T(8,128)(2,1)} %all-gather.19.cloned.1.call-done), kind=kOutput, calls=%fused_computation.118 | convolution fusion | flops 403439360 | bytes 2622464 | tf_op jit(solution)/shard_map/dot_general | solution.py:28
  129.4 0.8 copy.107
  (114 shorter events, 5.2 us)
Async XLA Ops:
  7.2 4.8 %copy-start = (s32[16,16,2]{1,2,0:T(2,128)S(1)}, s32[16,16,2]{1,2,0:T(2,128)}, u32[]{:S(2)}) copy-start(s32[16,16,2]{1,2,0:T(2,128)} %param.27) | copy-start | bytes 6148
  7.2 2.9 %copy-start.9 = (bf16[2,1024,256]{2,1,0:T(8,128)(2,1)S(1)}, bf16[2,1024,256]{2,1,0:T(8,128)(2,1)}, u32[]{:S(2)}) copy-start(bf16[2,1024,256]{2,1,0:T(8,128)(2,1)} %param.30) | copy-start | bytes 3145732
  7.2 55.9 %all-gather.13.cloned.1.call-start = ((), (), s32[]{:S(2)}) async-start(), calls=%async_computation.2 | async-start | bytes 2359296 | tf_op jit(solution)/shard_map/all_gather | solution.py:65
  10.0 2.2 %copy-start.1 = (bf16[2,128,512]{2,1,0:T(8,128)(2,1)S(1)}, bf16[2,128,512]{2,1,0:T(8,128)(2,1)}, u32[]{:S(2)}) copy-start(bf16[2,128,512]{2,1,0:T(8,128)(2,1)} %param.21) | copy-start | bytes 786436
  10.0 12.1 %copy-start.20 = (s32[32]{0:T(128)S(1)}, s32[32]{0:T(128)}, u32[]{:S(2)}) copy-start(s32[32]{0:T(128)} %param.26) | copy-start | bytes 388
  10.0 65.2 %all-gather.15.cloned.1.call-start = ((), (), s32[]{:S(2)}) async-start(), calls=%async_computation.3 | async-start | bytes 1572864 | tf_op jit(solution)/shard_map/all_gather | solution.py:67
  11.2 17.6 %copy-start.15 = (s32[512]{0:T(512)S(1)}, s32[512]{0:T(512)}, u32[]{:S(2)}) copy-start(s32[512]{0:T(512)} %param.23) | copy-start | bytes 6148
  11.2 17.6 %copy-start.14 = (s32[512]{0:T(512)S(1)}, s32[512]{0:T(512)}, u32[]{:S(2)}) copy-start(s32[512]{0:T(512)} %param.24) | copy-start | bytes 6148
  11.2 103.8 %all-gather.17.cloned.1.call-start = ((), (), s32[]{:S(2)}) async-start(), calls=%async_computation.4 | async-start | bytes 2359296 | tf_op jit(solution)/shard_map/all_gather | solution.py:65
  13.7 37.8 %all-to-all-start = ((bf16[2,32,512]{2,0,1:T(2,128)(2,1)}), bf16[2,32,512]{2,0,1:T(2,128)(2,1)S(1)}, u32[]{:S(2)}, u32[]{:S(2)}) async-start(bf16[2,32,512]{2,0,1:T(2,128)(2,1)} %copy.84), calls=%async_computation | async-start | bytes 131072 | tf_op jit(solution)/shard_map/all_to_all | solution.py:76
  22.1 104.0 %all-gather.19.cloned.1.call-start = ((), (), s32[]{:S(2)}) async-start(), calls=%async_computation.5 | async-start | bytes 1572864 | tf_op jit(solution)/shard_map/all_gather | solution.py:67
  23.0 28.3 %collective-permute-start = (bf16[2,16,512]{2,1,0:T(8,128)(2,1)S(1)}, bf16[2,16,512]{2,1,0:T(8,128)(2,1)S(1)}, u32[]{:S(2)}, u32[]{:S(2)}) collective-permute-start(bf16[2,16,512]{2,1,0:T(8,128)(2,1)S(1)} %get-tuple-element.23), channel_id=1, source_target_pairs={{0,2},{2,4},{4,6},{6,8},{8,10},{10,12},{12,14},{14,16},{16,18},{18... | collective-permute-start | bytes 98312 | tf_op jit(solution)/shard_map/ppermute | solution.py:16
  25.0 26.4 %collective-permute-start.1 = (bf16[2,16,512]{2,1,0:T(8,128)(2,1)S(1)}, bf16[2,16,512]{2,1,0:T(8,128)(2,1)S(1)}, u32[]{:S(2)}, u32[]{:S(2)}) collective-permute-start(bf16[2,16,512]{2,1,0:T(8,128)(2,1)S(1)} %get-tuple-element.24), channel_id=1, source_target_pairs={{2,0},{4,2},{6,4},{8,6},{10,8},{12,10},{14,12},{16,14},{18,16},{20... | collective-permute-start | bytes 98312 | tf_op jit(solution)/shard_map/ppermute | solution.py:19
  28.8 4.5 %copy-start.12 = (bf16[2,512,256]{2,1,0:T(8,128)(2,1)S(1)}, bf16[2,512,256]{2,1,0:T(8,128)(2,1)}, u32[]{:S(2)}) copy-start(bf16[2,512,256]{2,1,0:T(8,128)(2,1)} %param.29) | copy-start | bytes 1572868
  28.8 7.0 %copy-start.16 = (f32[2,512]{1,0:T(2,128)S(1)}, f32[2,512]{1,0:T(2,128)}, u32[]{:S(2)}) copy-start(f32[2,512]{1,0:T(2,128)} %param.32) | copy-start | bytes 12292
  28.8 7.0 %copy-start.17 = (f32[2,512]{1,0:T(2,128)S(1)}, f32[2,512]{1,0:T(2,128)}, u32[]{:S(2)}) copy-start(f32[2,512]{1,0:T(2,128)} %param.33) | copy-start | bytes 12292
  33.3 2.6 %copy-start.13 = (bf16[2,512,256]{2,1,0:T(8,128)(2,1)S(1)}, bf16[2,512,256]{2,1,0:T(8,128)(2,1)}, u32[]{:S(2)}) copy-start(bf16[2,512,256]{2,1,0:T(8,128)(2,1)} %param.31) | copy-start | bytes 1572868
  33.3 4.9 %copy-start.18 = (f32[2,512]{1,0:T(2,128)S(1)}, f32[2,512]{1,0:T(2,128)}, u32[]{:S(2)}) copy-start(f32[2,512]{1,0:T(2,128)} %param.34) | copy-start | bytes 12292
  33.3 4.9 %copy-start.19 = (f32[2,512]{1,0:T(2,128)S(1)}, f32[2,512]{1,0:T(2,128)}, u32[]{:S(2)}) copy-start(f32[2,512]{1,0:T(2,128)} %param.35) | copy-start | bytes 12292
  40.6 8.7 %copy-start.2 = (bf16[2,512,512]{2,1,0:T(8,128)(2,1)S(1)}, bf16[2,512,512]{2,1,0:T(8,128)(2,1)}, u32[]{:S(2)}) copy-start(bf16[2,512,512]{2,1,0:T(8,128)(2,1)} %param.22) | copy-start | bytes 3145732
  49.3 25.6 %copy-start.7 = (bf16[2,128,512]{1,2,0:T(8,128)(2,1)}, bf16[2,128,512]{1,2,0:T(8,128)(2,1)S(1)}, u32[]{:S(2)}) copy-start(bf16[2,128,512]{1,2,0:T(8,128)(2,1)S(1)} %copy.81) | copy-start | bytes 786436
  55.6 2.0 %copy-start.4 = (bf16[2,512,512]{2,0,1:T(2,128)(2,1)S(1)}, bf16[2,512,512]{2,0,1:T(2,128)(2,1)}, u32[]{:S(2)}) copy-start(bf16[2,512,512]{2,0,1:T(2,128)(2,1)} %fusion.29) | copy-start | bytes 3145732
  55.7 2.0 %copy-start.6 = (bf16[2,512,512]{2,0,1:T(2,128)(2,1)S(1)}, bf16[2,512,512]{2,0,1:T(2,128)(2,1)}, u32[]{:S(2)}) copy-start(bf16[2,512,512]{2,0,1:T(2,128)(2,1)} %copy.82) | copy-start | bytes 3145732
  74.4 1.0 copy-start.11
  77.5 1.0 copy-start.8
  84.7 17.6 %collective-permute-start.2 = (bf16[2,16,512]{1,2,0:T(8,128)(2,1)}, bf16[2,16,512]{1,2,0:T(8,128)(2,1)S(1)}, u32[]{:S(2)}, u32[]{:S(2)}) collective-permute-start(bf16[2,16,512]{1,2,0:T(8,128)(2,1)} %get-tuple-element.21), channel_id=1, source_target_pairs={{0,2},{2,4},{4,6},{6,8},{8,10},{10,12},{12,14},{14,16},{16,18},{18... | collective-permute-start | bytes 98312 | tf_op jit(solution)/shard_map/ppermute | solution.py:16
  84.7 17.6 %collective-permute-start.3 = (bf16[2,16,512]{1,2,0:T(8,128)(2,1)S(1)}, bf16[2,16,512]{1,2,0:T(8,128)(2,1)}, u32[]{:S(2)}, u32[]{:S(2)}) collective-permute-start(bf16[2,16,512]{1,2,0:T(8,128)(2,1)S(1)} %get-tuple-element.22), channel_id=1, source_target_pairs={{2,0},{4,2},{6,4},{8,6},{10,8},{12,10},{14,12},{16,14},{18,16},{20... | collective-permute-start | bytes 98312 | tf_op jit(solution)/shard_map/ppermute | solution.py:19
  91.1 11.0 %all-to-all-start.1 = ((bf16[2,32,512]{2,0,1:T(2,128)(2,1)}), bf16[2,32,512]{2,0,1:T(2,128)(2,1)S(1)}, u32[]{:S(2)}, u32[]{:S(2)}) async-start(bf16[2,32,512]{2,0,1:T(2,128)(2,1)} %fusion.55), calls=%async_computation.1 | async-start | bytes 131072 | tf_op jit(solution)/shard_map/all_to_all | solution.py:76
  107.6 2.0 %copy-start.5 = (bf16[2,512,512]{2,0,1:T(2,128)(2,1)S(1)}, bf16[2,512,512]{2,0,1:T(2,128)(2,1)}, u32[]{:S(2)}) copy-start(bf16[2,512,512]{2,0,1:T(2,128)(2,1)} %fusion.30) | copy-start | bytes 3145732
  125.3 3.4 %copy-start.3 = (bf16[2,512,512]{2,1,0:T(8,128)(2,1)}, bf16[2,512,512]{2,1,0:T(8,128)(2,1)S(1)}, u32[]{:S(2)}) copy-start(bf16[2,512,512]{2,1,0:T(8,128)(2,1)S(1)} %copy.108) | copy-start | bytes 3145732
  125.3 1.4 %copy-start.10 = (bf16[1,512,512]{2,1,0:T(8,128)(2,1)S(1)}, bf16[1,512,512]{2,1,0:T(8,128)(2,1)}, u32[]{:S(2)}) copy-start(bf16[1,512,512]{2,1,0:T(8,128)(2,1)} %all-gather.7) | copy-start | bytes 1572868
Sparse Core Ops, SparseCore 0:
  10.1 12.1 all-gather.12
  23.9 9.9 all-gather.14
  35.4 10.6 all-gather.16
  47.5 9.9 all-gather.18
where the time goes:
time: 137 us
  local copies, waits for them, and re-layouts  34.7 us (25%)
  other arithmetic  33.2 us (24%)
  starting transfers between devices  23.3 us (17%)
  between operations  15.2 us (11%)
  matrix products  15.1 us (11%)
  blocking collectives  9.69 us (7%)
  waiting for transfers between devices  5.66 us (4%)
    dot_general x4, matrix products, project_norm(): output = jnp.dot(hidden, second, preferred_element_type=jnp.float32)  14.1 us
    all_to_all x2, starting transfers between devices, per_device(): lax.all_to_all(packed, 'dom', split_axis=1, concat_axis=1, tiled=True)  11.8 us
    convert_element_type x2, other arithmetic, per_device(): new_edges = jnp.where(live_mask[None, :, None], edge_state.astype(jnp.flo...  9.73 us
    ppermute x2, starting transfers between devices, with_halo(): lax.ppermute(lax.slice_in_dim(block, 0, width, axis=dim), axis, backward)  9.32 us
    gather x2, local copies, waits for them, and re-layouts, per_device(): receiver_rows = jnp.take(node_state, edge_receivers, axis=1)  8 us
    select_n x3, other arithmetic, per_device(): receiver_rows = jnp.take(node_state, edge_receivers, axis=1)  7.59 us
    gather x2, local copies, waits for them, and re-layouts, per_device(): sender_rows = jnp.take(sources, edge_senders, axis=1)  7.11 us
    concatenate x2, other arithmetic, per_device(): joined = jnp.concatenate([edge_state, sender_rows, receiver_rows], -1)  6.59 us
  transfers between devices with their start and end apart: 10, of which 1 were waited for; matrix products, arithmetic and copies ran while one was open for 55% of the time, Pallas kernels for 0%

commit v1 on v0

--- a/solution.py
+++ b/solution.py
@@ -2,6 +2,7 @@
 import jax.numpy as jnp
 from jax import lax
 from jax.sharding import PartitionSpec as P
+from jax.lax import all_to_all, axis_size
 
 HALO = 16
 LAYERS = 2
@@ -73,7 +74,10 @@
         from_right = bordered[:, 3 * HALO :]
         send_rows = lax.dynamic_index_in_dim(long_send, position, 0, keepdims=False).reshape(-1)
         packed = jnp.take(node_state, send_rows, axis=1)
-        far_rows = lax.all_to_all(packed, "dom", split_axis=1, concat_axis=1, tiled=True)
+        reach_regions = lambda mine: jnp.concatenate(
+            all_to_all(jnp.stack(jnp.split(mine, axis_size("dom"), 1), 0), "dom", 0, 0), 1
+        )
+        far_rows = reach_regions(packed)
         sources = jnp.concatenate([node_state, from_left, from_right, far_rows], 1)
         sender_rows = jnp.take(sources, edge_senders, axis=1)
         receiver_rows = jnp.take(node_state, edge_receivers, axis=1)

time: 137 us -> 157 us (1.15)
  local copies, waits for them, and re-layouts: 34.7 us -> 53 us
  waiting for transfers between devices: 5.66 us -> 7.72 us
    unnamed x46 -> x76, local copies, waits for them, and re-layouts: 4.66 us -> 22.4 us
    ppermute x2, waiting for transfers between devices: 0.01 us -> 5.02 us  [with_halo(): lax.ppermute(lax.slice_in_dim(block, block.shape[dim] - width, None, axis...]
    all_to_all x2, waiting for transfers between devices: 4.88 us -> 0.01 us  [per_device(): all_to_all(jnp.stack(jnp.split(mine, axis_size('dom'), 1), 0), 'dom', 0, 0)]
    ppermute x2, starting transfers between devices: 9.32 us -> 7.4 us  [with_halo(): lax.ppermute(lax.slice_in_dim(block, 0, width, axis=dim), axis, backward)]
    ppermute x2, starting transfers between devices: 1.98 us -> 3.9 us  [with_halo(): lax.ppermute(lax.slice_in_dim(block, block.shape[dim] - width, None, axis...]
    ppermute x2, waiting for transfers between devices: 0.01 us -> 1.92 us  [with_halo(): lax.ppermute(lax.slice_in_dim(block, 0, width, axis=dim), axis, backward)]
  transfers between devices with their start and end apart: 10 -> 10, of which waited for: 1 -> 2; matrix products, arithmetic and copies ran while one was open for 55% -> 59% of each run, Pallas kernels for 0% -> 0%
where the time goes in v1:
time: 157 us
  local copies, waits for them, and re-layouts  53 us (34%)
  other arithmetic  32.5 us (21%)
  starting transfers between devices  23.5 us (15%)
  between operations  15.2 us (10%)
  matrix products  15.1 us (10%)
  blocking collectives  9.69 us (6%)
  waiting for transfers between devices  7.72 us (5%)
    unnamed x76, local copies, waits for them, and re-layouts  22.4 us
    dot_general x4, matrix products, project_norm(): output = jnp.dot(hidden, second, preferred_element_type=jnp.float32)  14.1 us
    all_to_all x2, starting transfers between devices, per_device(): all_to_all(jnp.stack(jnp.split(mine, axis_size('dom'), 1), 0), 'dom', 0, 0)  12 us
    convert_element_type x2, other arithmetic, per_device(): new_edges = jnp.where(live_mask[None, :, None], edge_state.astype(jnp.flo...  9.73 us
    gather x2, local copies, waits for them, and re-layouts, per_device(): receiver_rows = jnp.take(node_state, edge_receivers, axis=1)  8 us
    select_n x3, other arithmetic, per_device(): receiver_rows = jnp.take(node_state, edge_receivers, axis=1)  7.56 us
    ppermute x2, starting transfers between devices, with_halo(): lax.ppermute(lax.slice_in_dim(block, 0, width, axis=dim), axis, backward)  7.4 us
    gather x2, local copies, waits for them, and re-layouts, per_device(): sender_rows = jnp.take(sources, edge_senders, axis=1)  7.11 us
  transfers between devices with their start and end apart: 10, of which 2 were waited for; matrix products, arithmetic and copies ran while one was open for 59% of the time, Pallas kernels for 0%

profile of v1, /device:TPU:0, one launch (start us, length us, event | category | flops | bytes accessed | tf_op | source)
XLA Modules:
  0.0 156.7 jit_solution(93415451599617697)
XLA Ops:
  7.2 2.7 %fusion.60 = (bf16[1,1536,256]{2,1,0:T(8,128)(2,1)}, bf16[1,1536,256]{2,1,0:T(8,128)(2,1)}) fusion(bf16[2,1536,256]{2,1,0:T(8,128)(2,1)} %param.28), kind=kLoop, calls=%fused_computation.169 | loop fusion | bytes 3145728 | tf_op jit(solution)/shard_map/slice | solution.py:66
  10.1 1.1 fusion.61
  11.2 0.7 all-gather.17.cloned.1.call-update
  12.2 0.8 gather_fusion.1
  13.1 0.6 constant_dynamic-update-slice_fusion.15
  16.0 0.6 constant_dynamic-update-slice_fusion.10
  19.0 0.6 constant_dynamic-update-slice_fusion.5
  22.0 0.6 constant_dynamic-update-slice_fusion
  22.6 8.3 %all-to-all-start = ((bf16[16,2,2,512]{3,2,1,0:T(2,128)(2,1)}), bf16[16,2,2,512]{3,2,1,0:T(2,128)(2,1)S(1)}, u32[]{:S(2)}, u32[]{:S(2)}) async-start(bf16[16,2,2,512]{3,2,1,0:T(2,128)(2,1)} %constant_dynamic-update-slice_fusion), calls=%async_computation | async-start | bytes 131072 | tf_op jit(solution)/shard_map/all_to_all | solution.py:78
  31.0 0.8 gather_fusion
  31.9 2.0 %collective-permute-start = (bf16[2,16,512]{2,1,0:T(8,128)(2,1)S(1)}, bf16[2,16,512]{2,1,0:T(8,128)(2,1)S(1)}, u32[]{:S(2)}, u32[]{:S(2)}) collective-permute-start(bf16[2,16,512]{2,1,0:T(8,128)(2,1)S(1)} %get-tuple-element.21), channel_id=1, source_target_pairs={{0,2},{2,4},{4,6},{6,8},{8,10},{10,12},{12,14},{14,16},{16,18},{18... | collective-permute-start | bytes 98312 | tf_op jit(solution)/shard_map/ppermute | solution.py:17
  33.9 3.7 %collective-permute-start.1 = (bf16[2,16,512]{2,1,0:T(8,128)(2,1)S(1)}, bf16[2,16,512]{2,1,0:T(8,128)(2,1)S(1)}, u32[]{:S(2)}, u32[]{:S(2)}) collective-permute-start(bf16[2,16,512]{2,1,0:T(8,128)(2,1)S(1)} %get-tuple-element.22), channel_id=1, source_target_pairs={{2,0},{4,2},{6,4},{8,6},{10,8},{12,10},{14,12},{16,14},{18,16},{20... | collective-permute-start | bytes 98312 | tf_op jit(solution)/shard_map/ppermute | solution.py:20
  37.7 4.4 %gather_fusion.3 = bf16[512,2,512]{2,0,1:T(8,128)(2,1)S(1)} fusion(bf16[2,128,512]{2,1,0:T(8,128)(2,1)S(1)} %copy-done.1, s32[1024]{0:T(1024)S(1)} %get-tuple-element.39), kind=kCustom, calls=%fused_computation.2.clone | custom fusion | bytes 2099200 | tf_op jit(solution)/shard_map/jit(_take)/gather | solution.py:83
  42.2 2.4 %all-gather.1 = bf16[1,512,512]{2,1,0:T(8,128)(2,1)} all-gather(bf16[1,512,256]{2,1,0:T(8,128)(2,1)S(1)} %get-tuple-element.16), channel_id=3, replica_groups=mesh['dom'=16,'mem'=2] {'mem'}, dimensions={2}, use_global_device_ids=true | all-gather | bytes 786432 | tf_op jit(solution)/shard_map/all_gather | solution.py:67
  44.7 2.3 %all-gather.3 = bf16[1,512,512]{2,1,0:T(8,128)(2,1)} all-gather(bf16[1,512,256]{2,1,0:T(8,128)(2,1)S(1)} %get-tuple-element.17), channel_id=5, replica_groups=mesh['dom'=16,'mem'=2] {'mem'}, dimensions={2}, use_global_device_ids=true | all-gather | bytes 786432 | tf_op jit(solution)/shard_map/all_gather | solution.py:69
  47.1 2.3 %all-gather.5 = bf16[1,512,512]{2,1,0:T(8,128)(2,1)} all-gather(bf16[1,512,256]{2,1,0:T(8,128)(2,1)S(1)} %get-tuple-element.15), channel_id=7, replica_groups=mesh['dom'=16,'mem'=2] {'mem'}, dimensions={2}, use_global_device_ids=true | all-gather | bytes 786432 | tf_op jit(solution)/shard_map/all_gather | solution.py:67
  49.4 2.6 %all-gather.7 = bf16[1,512,512]{2,1,0:T(8,128)(2,1)} all-gather(bf16[1,512,256]{2,1,0:T(8,128)(2,1)S(1)} %get-tuple-element.18), channel_id=9, replica_groups=mesh['dom'=16,'mem'=2] {'mem'}, dimensions={2}, use_global_device_ids=true | all-gather | bytes 786432 | tf_op jit(solution)/shard_map/all_gather | solution.py:69
  52.0 5.0 %fusion.29 = bf16[2,512,512]{2,0,1:T(2,128)(2,1)} fusion(bf16[512,2,512]{2,0,1:T(8,128)(2,1)S(1)} %gather_fusion.3, pred[512]{0:T(512)(128)(4,1)S(1)} %compare_and_fusion), kind=kLoop, calls=%fused_computation.45 | loop fusion | flops 524288 | bytes 2097664 | tf_op jit(solution)/shard_map/jit(_take)/select_n | solution.py:83
  58.1 2.1 %copy.55 = bf16[2,512,512]{2,0,1:T(2,128)(2,1)} copy(bf16[2,512,512]{2,1,0:T(8,128)(2,1)S(1)} %copy-done.2) | data formatting | bytes 2097152 | tf_op args[1]
  61.0 3.6 %gather_fusion.2 = bf16[512,2,512]{2,1,0:T(2,128)(2,1)S(1)} fusion(bf16[2,192,512]{2,0,1:T(2,128)(2,1)S(1)} %pad_maximum_fusion.5, s32[1024]{0:T(1024)S(1)} %pad_clamp_fusion.1), kind=kCustom, calls=%fused_computation.1.clone | custom fusion | bytes 2099200 | tf_op jit(solution)/shard_map/jit(_take)/gather | solution.py:82
  64.5 2.0 %fusion.27 = bf16[2,512,512]{2,0,1:T(2,128)(2,1)S(1)} fusion(bf16[512,2,512]{2,1,0:T(2,128)(2,1)S(1)} %gather_fusion.2, pred[512]{0:T(512)(128)(4,1)S(1)} %compare_and_fusion.1), kind=kLoop, calls=%fused_computation.43 | loop fusion | flops 524288 | bytes 2097664 | tf_op jit(solution)/shard_map/jit(_take)/select_n | solution.py:82
  66.5 3.3 %pad_maximum_fusion = bf16[2,512,1536]{2,0,1:T(2,128)(2,1)S(1)} fusion(bf16[2,512,512]{2,0,1:T(2,128)(2,1)S(1)} %copy-done.4, bf16[2,512,512]{2,0,1:T(2,128)(2,1)S(1)} %fusion.27, bf16[2,512,512]{2,0,1:T(2,128)(2,1)S(1)} %copy-done.6), kind=kLoop, calls=%fused_computation.8 | loop fusion | flops 9437184 | bytes 6291456 | tf_op jit(solution)/shard_map/concatenate | solution.py:84
  69.8 2.1 %copy.63 = bf16[2,512,1536]{2,1,0:T(8,128)(2,1)} copy(bf16[2,512,1536]{2,0,1:T(2,128)(2,1)S(1)} %pad_maximum_fusion) | data formatting | bytes 6291456 | tf_op jit(solution)/shard_map/concatenate | solution.py:84
  72.0 5.0 %fusion.70 = (f32[1024]{0:T(1024)S(1)}, f32[1024,512]{1,0:T(8,128)S(1)}) fusion(bf16[1,512,512]{2,1,0:T(8,128)(2,1)} %all-gather.1, bf16[1024,1536]{1,0:T(8,128)(2,1)} %bitcast.238, bf16[1,1536,512]{2,1,0:T(8,128)(2,1)} %all-gather.13.cloned.1.call-done), kind=kOutput, calls=%fused_computation.179 | convolution fusion | flops 2150628352 | bytes 7344128 | tf_op jit(solution)/shard_map/dot_general | solution.py:29
  77.8 5.5 %fusion.3 = bf16[2,512,512]{2,0,1:T(2,128)(2,1)S(1)} fusion(f32[2,512,512]{2,1,0:T(8,128)S(1)} %bitcast.237, pred[512]{0:T(512)(128)(4,1)S(1)} %iota_compare_fusion.1, bf16[2,512,512]{2,1,0:T(8,128)(2,1)S(1)} %copy-done.2), kind=kLoop, calls=%fused_computation.15 | loop fusion | flops 2097152 | bytes 4194816 | tf_op jit(solution)/shard_map/convert_element_type | solution.py:94
  84.3 2.0 %fusion.73 = (f32[256]{0:T(256)S(1)}, f32[256,512]{1,0:T(8,128)S(1)}) fusion(bf16[1,512,512]{2,1,0:T(8,128)(2,1)S(1)} %copy-done.11, bf16[256,1024]{1,0:T(8,128)(2,1)S(1)} %bitcast.242, bf16[1,1024,512]{2,1,0:T(8,128)(2,1)} %all-gather.15.cloned.1.call-done), kind=kOutput, calls=%fused_computation.180 | convolution fusion | flops 403439360 | bytes 2622464 | tf_op jit(solution)/shard_map/dot_general | solution.py:29
  87.5 0.7 gather_fusion.5
  88.2 0.7 gather_fusion.4
  88.9 3.6 %gather_fusion.7 = bf16[512,2,512]{2,1,0:T(2,128)(2,1)S(1)} fusion(bf16[2,128,512]{2,0,1:T(2,128)(2,1)S(1)} %copy.69, s32[1024]{0:T(1024)S(1)} %get-tuple-element.39), kind=kCustom, calls=%fused_computation.7.clone | custom fusion | bytes 2099200 | tf_op jit(solution)/shard_map/jit(_take)/gather | solution.py:83
  93.8 0.6 constant_dynamic-update-slice_fusion.29
  100.3 0.6 constant_dynamic-update-slice_fusion.18
  102.1 3.7 %all-to-all-start.1 = ((bf16[16,2,2,512]{3,1,2,0:T(2,128)(2,1)}), bf16[16,2,2,512]{3,1,2,0:T(2,128)(2,1)S(1)}, u32[]{:S(2)}, u32[]{:S(2)}) async-start(bf16[16,2,2,512]{3,1,2,0:T(2,128)(2,1)} %constant_dynamic-update-slice_fusion.16), calls=%async_computation.1 | async-start | bytes 131072 | tf_op jit(solution)/shard_map/all_to_all | solution.py:78
  106.1 0.8 fusion.64
  106.9 1.9 %collective-permute-start.2 = (bf16[2,16,512]{1,2,0:T(8,128)(2,1)}, bf16[2,16,512]{1,2,0:T(8,128)(2,1)S(1)}, u32[]{:S(2)}, u32[]{:S(2)}) collective-permute-start(bf16[2,16,512]{1,2,0:T(8,128)(2,1)} %get-tuple-element.19), channel_id=1, source_target_pairs={{0,2},{2,4},{4,6},{6,8},{8,10},{10,12},{12,14},{14,16},{16,18},{18... | collective-permute-start | bytes 98312 | tf_op jit(solution)/shard_map/ppermute | solution.py:17
  108.8 3.7 %collective-permute-start.3 = (bf16[2,16,512]{1,2,0:T(8,128)(2,1)S(1)}, bf16[2,16,512]{1,2,0:T(8,128)(2,1)}, u32[]{:S(2)}, u32[]{:S(2)}) collective-permute-start(bf16[2,16,512]{1,2,0:T(8,128)(2,1)S(1)} %get-tuple-element.20), channel_id=1, source_target_pairs={{2,0},{4,2},{6,4},{8,6},{10,8},{12,10},{14,12},{16,14},{18,16},{20... | collective-permute-start | bytes 98312 | tf_op jit(solution)/shard_map/ppermute | solution.py:20
  112.5 2.6 %fusion.30 = bf16[2,512,512]{2,0,1:T(2,128)(2,1)} fusion(bf16[512,2,512]{2,1,0:T(2,128)(2,1)S(1)} %gather_fusion.7, pred[512]{0:T(512)(128)(4,1)S(1)} %compare_and_fusion), kind=kLoop, calls=%fused_computation.46 | loop fusion | flops 524288 | bytes 2097664 | tf_op jit(solution)/shard_map/jit(_take)/select_n | solution.py:83
  115.3 5.0 %collective-permute-done.2 = bf16[2,16,512]{1,2,0:T(8,128)(2,1)S(1)} collective-permute-done((bf16[2,16,512]{1,2,0:T(8,128)(2,1)}, bf16[2,16,512]{1,2,0:T(8,128)(2,1)S(1)}, u32[]{:S(2)}, u32[]{:S(2)}) %collective-permute-start.2) | collective-permute-done | bytes 32800 | tf_op jit(solution)/shard_map/ppermute | solution.py:17
  120.3 1.9 %collective-permute-done.3 = bf16[2,16,512]{1,2,0:T(8,128)(2,1)} collective-permute-done((bf16[2,16,512]{1,2,0:T(8,128)(2,1)S(1)}, bf16[2,16,512]{1,2,0:T(8,128)(2,1)}, u32[]{:S(2)}, u32[]{:S(2)}) %collective-permute-start.3) | collective-permute-done | bytes 32800 | tf_op jit(solution)/shard_map/ppermute | solution.py:20
  122.3 1.2 pad_maximum_fusion.3
  124.0 3.6 %gather_fusion.6 = bf16[512,2,512]{2,1,0:T(2,128)(2,1)S(1)} fusion(bf16[2,192,512]{2,0,1:T(2,128)(2,1)S(1)} %copy.73, s32[1024]{0:T(1024)S(1)} %pad_clamp_fusion.1), kind=kCustom, calls=%fused_computation.6.clone | custom fusion | bytes 2099200 | tf_op jit(solution)/shard_map/jit(_take)/gather | solution.py:82
  127.5 2.0 %fusion.28 = bf16[2,512,512]{2,0,1:T(2,128)(2,1)S(1)} fusion(bf16[512,2,512]{2,1,0:T(2,128)(2,1)S(1)} %gather_fusion.6, pred[512]{0:T(512)(128)(4,1)S(1)} %compare_and_fusion.1), kind=kLoop, calls=%fused_computation.44 | loop fusion | flops 524288 | bytes 2097664 | tf_op jit(solution)/shard_map/jit(_take)/select_n | solution.py:82
  129.5 3.3 %pad_maximum_fusion.1 = bf16[2,512,1536]{2,0,1:T(2,128)(2,1)S(1)} fusion(bf16[2,512,512]{2,0,1:T(2,128)(2,1)S(1)} %copy-done.5, bf16[2,512,512]{2,0,1:T(2,128)(2,1)S(1)} %fusion.28, bf16[2,512,512]{2,0,1:T(2,128)(2,1)S(1)} %fusion.3), kind=kLoop, calls=%fused_computation.9 | loop fusion | flops 9437184 | bytes 6291456 | tf_op jit(solution)/shard_map/concatenate | solution.py:84
  132.8 2.1 %copy.75 = bf16[2,512,1536]{2,1,0:T(8,128)(2,1)} copy(bf16[2,512,1536]{2,0,1:T(2,128)(2,1)S(1)} %pad_maximum_fusion.1) | data formatting | bytes 6291456 | tf_op jit(solution)/shard_map/concatenate | solution.py:84
  134.9 5.0 %fusion.76 = (f32[1024]{0:T(1024)S(1)}, f32[1024,512]{1,0:T(8,128)S(1)}) fusion(bf16[1,512,512]{2,1,0:T(8,128)(2,1)} %all-gather.5, bf16[1024,1536]{1,0:T(8,128)(2,1)} %bitcast.239, bf16[1,1536,512]{2,1,0:T(8,128)(2,1)} %all-gather.17.cloned.1.call-done), kind=kOutput, calls=%fused_computation.181 | convolution fusion | flops 2150628352 | bytes 7344128 | tf_op jit(solution)/shard_map/dot_general | solution.py:29
  140.8 4.3 %fusion.1 = bf16[2,512,512]{2,0,1:T(2,128)(2,1)S(1)} fusion(f32[2,512,512]{2,1,0:T(8,128)S(1)} %bitcast.236, bf16[2,512,512]{2,0,1:T(2,128)(2,1)S(1)} %fusion.3, pred[512]{0:T(512)(128)(4,1)S(1)} %iota_compare_fusion.1), kind=kLoop, calls=%fused_computation.12 | loop fusion | flops 2097152 | bytes 4194816 | tf_op jit(solution)/shard_map/convert_element_type | solution.py:94
  146.0 0.6 copy-done.10
  146.7 2.0 %fusion.79 = (f32[256]{0:T(256)S(1)}, f32[256,512]{1,0:T(8,128)S(1)}) fusion(bf16[1,512,512]{2,1,0:T(8,128)(2,1)S(1)} %copy-done.10, bf16[256,1024]{1,0:T(8,128)(2,1)S(1)} %bitcast.243, bf16[1,1024,512]{2,1,0:T(8,128)(2,1)} %all-gather.19.cloned.1.call-done), kind=kOutput, calls=%fused_computation.182 | convolution fusion | flops 403439360 | bytes 2622464 | tf_op jit(solution)/shard_map/dot_general | solution.py:29
  149.4 0.8 copy.80
  (145 shorter events, 23.7 us)
Async XLA Ops:
  7.2 4.8 %copy-start = (s32[16,16,2]{1,2,0:T(2,128)S(1)}, s32[16,16,2]{1,2,0:T(2,128)}, u32[]{:S(2)}) copy-start(s32[16,16,2]{1,2,0:T(2,128)} %param.27) | copy-start | bytes 6148
  7.2 2.9 %copy-start.9 = (bf16[2,1024,256]{2,1,0:T(8,128)(2,1)S(1)}, bf16[2,1024,256]{2,1,0:T(8,128)(2,1)}, u32[]{:S(2)}) copy-start(bf16[2,1024,256]{2,1,0:T(8,128)(2,1)} %param.30) | copy-start | bytes 3145732
  7.2 64.8 %all-gather.13.cloned.1.call-start = ((), (), s32[]{:S(2)}) async-start(), calls=%async_computation.2 | async-start | bytes 2359296 | tf_op jit(solution)/shard_map/all_gather | solution.py:66
  10.0 2.2 %copy-start.14 = (s32[512]{0:T(512)S(1)}, s32[512]{0:T(512)}, u32[]{:S(2)}) copy-start(s32[512]{0:T(512)} %param.24) | copy-start | bytes 6148
  10.0 2.2 %copy-start.1 = (bf16[2,128,512]{2,1,0:T(8,128)(2,1)S(1)}, bf16[2,128,512]{2,1,0:T(8,128)(2,1)}, u32[]{:S(2)}) copy-start(bf16[2,128,512]{2,1,0:T(8,128)(2,1)} %param.21) | copy-start | bytes 786436
  10.0 21.0 %copy-start.20 = (s32[32]{0:T(128)S(1)}, s32[32]{0:T(128)}, u32[]{:S(2)}) copy-start(s32[32]{0:T(128)} %param.26) | copy-start | bytes 388
  10.0 74.1 %all-gather.15.cloned.1.call-start = ((), (), s32[]{:S(2)}) async-start(), calls=%async_computation.3 | async-start | bytes 1572864 | tf_op jit(solution)/shard_map/all_gather | solution.py:68
  11.2 26.4 %copy-start.15 = (s32[512]{0:T(512)S(1)}, s32[512]{0:T(512)}, u32[]{:S(2)}) copy-start(s32[512]{0:T(512)} %param.23) | copy-start | bytes 6148
  11.2 123.8 %all-gather.17.cloned.1.call-start = ((), (), s32[]{:S(2)}) async-start(), calls=%async_computation.4 | async-start | bytes 2359296 | tf_op jit(solution)/shard_map/all_gather | solution.py:66
  22.6 37.7 %all-to-all-start = ((bf16[16,2,2,512]{3,2,1,0:T(2,128)(2,1)}), bf16[16,2,2,512]{3,2,1,0:T(2,128)(2,1)S(1)}, u32[]{:S(2)}, u32[]{:S(2)}) async-start(bf16[16,2,2,512]{3,2,1,0:T(2,128)(2,1)} %constant_dynamic-update-slice_fusion), calls=%async_computation | async-start | bytes 131072 | tf_op jit(solution)/shard_map/all_to_all | solution.py:78
  30.9 115.1 %all-gather.19.cloned.1.call-start = ((), (), s32[]{:S(2)}) async-start(), calls=%async_computation.5 | async-start | bytes 1572864 | tf_op jit(solution)/shard_map/all_gather | solution.py:68
  31.9 28.3 %collective-permute-start = (bf16[2,16,512]{2,1,0:T(8,128)(2,1)S(1)}, bf16[2,16,512]{2,1,0:T(8,128)(2,1)S(1)}, u32[]{:S(2)}, u32[]{:S(2)}) collective-permute-start(bf16[2,16,512]{2,1,0:T(8,128)(2,1)S(1)} %get-tuple-element.21), channel_id=1, source_target_pairs={{0,2},{2,4},{4,6},{6,8},{8,10},{10,12},{12,14},{14,16},{16,18},{18... | collective-permute-start | bytes 98312 | tf_op jit(solution)/shard_map/ppermute | solution.py:17
  33.9 26.4 %collective-permute-start.1 = (bf16[2,16,512]{2,1,0:T(8,128)(2,1)S(1)}, bf16[2,16,512]{2,1,0:T(8,128)(2,1)S(1)}, u32[]{:S(2)}, u32[]{:S(2)}) collective-permute-start(bf16[2,16,512]{2,1,0:T(8,128)(2,1)S(1)} %get-tuple-element.22), channel_id=1, source_target_pairs={{2,0},{4,2},{6,4},{8,6},{10,8},{12,10},{14,12},{16,14},{18,16},{20... | collective-permute-start | bytes 98312 | tf_op jit(solution)/shard_map/ppermute | solution.py:20
  37.6 4.5 %copy-start.12 = (bf16[2,512,256]{2,1,0:T(8,128)(2,1)S(1)}, bf16[2,512,256]{2,1,0:T(8,128)(2,1)}, u32[]{:S(2)}) copy-start(bf16[2,512,256]{2,1,0:T(8,128)(2,1)} %param.29) | copy-start | bytes 1572868
  37.6 7.0 %copy-start.16 = (f32[2,512]{1,0:T(2,128)S(1)}, f32[2,512]{1,0:T(2,128)}, u32[]{:S(2)}) copy-start(f32[2,512]{1,0:T(2,128)} %param.32) | copy-start | bytes 12292
  37.7 7.0 %copy-start.17 = (f32[2,512]{1,0:T(2,128)S(1)}, f32[2,512]{1,0:T(2,128)}, u32[]{:S(2)}) copy-start(f32[2,512]{1,0:T(2,128)} %param.33) | copy-start | bytes 12292
  42.1 2.6 %copy-start.13 = (bf16[2,512,256]{2,1,0:T(8,128)(2,1)S(1)}, bf16[2,512,256]{2,1,0:T(8,128)(2,1)}, u32[]{:S(2)}) copy-start(bf16[2,512,256]{2,1,0:T(8,128)(2,1)} %param.31) | copy-start | bytes 1572868
  42.1 4.9 %copy-start.18 = (f32[2,512]{1,0:T(2,128)S(1)}, f32[2,512]{1,0:T(2,128)}, u32[]{:S(2)}) copy-start(f32[2,512]{1,0:T(2,128)} %param.34) | copy-start | bytes 12292
  42.2 4.9 %copy-start.19 = (f32[2,512]{1,0:T(2,128)S(1)}, f32[2,512]{1,0:T(2,128)}, u32[]{:S(2)}) copy-start(f32[2,512]{1,0:T(2,128)} %param.35) | copy-start | bytes 12292
  49.4 8.7 %copy-start.2 = (bf16[2,512,512]{2,1,0:T(8,128)(2,1)S(1)}, bf16[2,512,512]{2,1,0:T(8,128)(2,1)}, u32[]{:S(2)}) copy-start(bf16[2,512,512]{2,1,0:T(8,128)(2,1)} %param.22) | copy-start | bytes 3145732
  58.1 25.7 %copy-start.7 = (bf16[2,128,512]{1,2,0:T(8,128)(2,1)}, bf16[2,128,512]{1,2,0:T(8,128)(2,1)S(1)}, u32[]{:S(2)}) copy-start(bf16[2,128,512]{1,2,0:T(8,128)(2,1)S(1)} %copy.54) | copy-start | bytes 786436
  64.5 2.0 %copy-start.4 = (bf16[2,512,512]{2,0,1:T(2,128)(2,1)S(1)}, bf16[2,512,512]{2,0,1:T(2,128)(2,1)}, u32[]{:S(2)}) copy-start(bf16[2,512,512]{2,0,1:T(2,128)(2,1)} %fusion.29) | copy-start | bytes 3145732
  64.5 2.0 %copy-start.6 = (bf16[2,512,512]{2,0,1:T(2,128)(2,1)S(1)}, bf16[2,512,512]{2,0,1:T(2,128)(2,1)}, u32[]{:S(2)}) copy-start(bf16[2,512,512]{2,0,1:T(2,128)(2,1)} %copy.55) | copy-start | bytes 3145732
  83.3 1.0 copy-start.11
  86.3 1.0 copy-start.8
  102.1 13.0 %all-to-all-start.1 = ((bf16[16,2,2,512]{3,1,2,0:T(2,128)(2,1)}), bf16[16,2,2,512]{3,1,2,0:T(2,128)(2,1)S(1)}, u32[]{:S(2)}, u32[]{:S(2)}) async-start(bf16[16,2,2,512]{3,1,2,0:T(2,128)(2,1)} %constant_dynamic-update-slice_fusion.16), calls=%async_computation.1 | async-start | bytes 131072 | tf_op jit(solution)/shard_map/all_to_all | solution.py:78
  106.9 13.4 %collective-permute-start.2 = (bf16[2,16,512]{1,2,0:T(8,128)(2,1)}, bf16[2,16,512]{1,2,0:T(8,128)(2,1)S(1)}, u32[]{:S(2)}, u32[]{:S(2)}) collective-permute-start(bf16[2,16,512]{1,2,0:T(8,128)(2,1)} %get-tuple-element.19), channel_id=1, source_target_pairs={{0,2},{2,4},{4,6},{6,8},{8,10},{10,12},{12,14},{14,16},{16,18},{18... | collective-permute-start | bytes 98312 | tf_op jit(solution)/shard_map/ppermute | solution.py:17
  108.8 13.4 %collective-permute-start.3 = (bf16[2,16,512]{1,2,0:T(8,128)(2,1)S(1)}, bf16[2,16,512]{1,2,0:T(8,128)(2,1)}, u32[]{:S(2)}, u32[]{:S(2)}) collective-permute-start(bf16[2,16,512]{1,2,0:T(8,128)(2,1)S(1)} %get-tuple-element.20), channel_id=1, source_target_pairs={{2,0},{4,2},{6,4},{8,6},{10,8},{12,10},{14,12},{16,14},{18,16},{20... | collective-permute-start | bytes 98312 | tf_op jit(solution)/shard_map/ppermute | solution.py:20
  127.5 2.0 %copy-start.5 = (bf16[2,512,512]{2,0,1:T(2,128)(2,1)S(1)}, bf16[2,512,512]{2,0,1:T(2,128)(2,1)}, u32[]{:S(2)}) copy-start(bf16[2,512,512]{2,0,1:T(2,128)(2,1)} %fusion.30) | copy-start | bytes 3145732
  145.2 3.5 %copy-start.3 = (bf16[2,512,512]{2,1,0:T(8,128)(2,1)}, bf16[2,512,512]{2,1,0:T(8,128)(2,1)S(1)}, u32[]{:S(2)}) copy-start(bf16[2,512,512]{2,1,0:T(8,128)(2,1)S(1)} %copy.81) | copy-start | bytes 3145732
  145.3 1.4 copy-start.10
Sparse Core Ops, SparseCore 0:
  10.1 12.1 all-gather.12
  23.9 9.9 all-gather.14
  35.4 10.6 all-gather.16
  47.5 10.3 all-gather.18
